TPU v7x, 32 devices: a whole 2x2x4 slice. The times are simulated.
32 devices in a mesh: pr: 8 (over y, x, core), pc: 4 (over z).
Axes of the slice: x: 2, y: 2, z: 4, core: 2. Of those that a mesh axis runs over, the one named last changes fastest.
Arguments:
- pair_array: bfloat16 [256, 256, 128], P('pr', 'pc'), may hold values from -6 to 6
- left_weight: bfloat16 [128, 128], replicated, may hold values from -0.5 to 0.5
- right_weight: bfloat16 [128, 128], replicated, may hold values from -0.5 to 0.5
- left_gate: bfloat16 [128, 128], replicated, may hold values from -0.5 to 0.5
- right_gate: bfloat16 [128, 128], replicated, may hold values from -0.5 to 0.5
- mid_gain: float32 [128], replicated, may hold values from 0.25 to 1.75
- out_weight: bfloat16 [128, 128], replicated, may hold values from -0.5 to 0.5
- out_gate: bfloat16 [128, 128], replicated, may hold values from -0.5 to 0.5
Outputs:
- pair_update: bfloat16 [256, 256, 128], P('pr', 'pc')
All inputs are finite; a program needn't handle non-finite values.
Results may differ from a plain program's by a relative error of at most 0.012.
Values may be sent and summed in bfloat16 or wider, within the bound.
A program may use at most 128 MiB of HBM per device.

v0:
```python
import jax
import jax.numpy as jnp
from jax import lax
from jax.sharding import PartitionSpec as P


def unit_channels(values, channel_gain):
    centred = values - jnp.mean(values, axis=-1, keepdims=True)
    return (
        centred
        * lax.rsqrt(jnp.mean(centred * centred, axis=-1, keepdims=True) + 1e-05)
        * channel_gain
    )


def make_factors(pair_in, left_weight, right_weight, left_gate, right_gate):
    left = jnp.einsum("ijc,cd->ijd", pair_in, left_weight, preferred_element_type=jnp.float32)
    left = left * jax.nn.sigmoid(
        jnp.einsum("ijc,cd->ijd", pair_in, left_gate, preferred_element_type=jnp.float32)
    )
    right = jnp.einsum("ijc,cd->ijd", pair_in, right_weight, preferred_element_type=jnp.float32)
    right = right * jax.nn.sigmoid(
        jnp.einsum("ijc,cd->ijd", pair_in, right_gate, preferred_element_type=jnp.float32)
    )
    return (pair_in, left.astype(jnp.bfloat16), right.astype(jnp.bfloat16))


def to_pair(mixed, ready, mid_gain, out_weight, out_gate):
    scaled = unit_channels(mixed.astype(jnp.float32), mid_gain).astype(jnp.bfloat16)
    scaled = lax.optimization_barrier(scaled)
    gate = jax.nn.sigmoid(
        jnp.einsum("ijc,cd->ijd", ready, out_gate, preferred_element_type=jnp.float32)
    )
    return (
        jnp.einsum("ijd,dc->ijc", scaled, out_weight, preferred_element_type=jnp.float32) * gate
    ).astype(jnp.bfloat16)


def on_device(
    pair_array, left_weight, right_weight, left_gate, right_gate, mid_gain, out_weight, out_gate
):
    ready, left, right = make_factors(pair_array, left_weight, right_weight, left_gate, right_gate)
    count = pair_array.shape[0] * lax.axis_size("pr")
    left_lines, right_lines = (
        lax.all_to_all(left, "pr", split_axis=2, concat_axis=0, tiled=True),
        lax.all_to_all(right, "pr", split_axis=2, concat_axis=0, tiled=True),
    )
    strip = jnp.einsum(
        "kid,kjd->ijd",
        lax.all_gather(left_lines, "pc", axis=1, tiled=True),
        right_lines,
        preferred_element_type=jnp.float32,
    )
    strip = (strip * count ** (-0.5)).astype(jnp.bfloat16)
    mixed = lax.all_to_all(strip, "pr", split_axis=0, concat_axis=2, tiled=True)
    return to_pair(mixed, ready, mid_gain, out_weight, out_gate)


def solution(mesh):
    return jax.shard_map(
        on_device,
        mesh=mesh,
        in_specs=(P("pr", "pc", None), P(), P(), P(), P(), P(), P(), P()),
        out_specs=P("pr", "pc", None),
        check_vma=False,
    )
```

profile of v0, /device:TPU:0, one launch (start us, length us, event | category | flops | bytes accessed | tf_op | source)
XLA Modules:
  0.0 104.0 jit_solution(1541400130074911763)
XLA Ops:
  6.5 0.0 copy-start
  6.5 0.0 all-gather.2.cloned.1.call-start
  6.5 1.0 copy-done
  7.6 1.0 fusion.24
  8.6 1.2 %fusion.14 = bf16[32,64,128]{2,1,0:T(8,128)(2,1)S(1)} fusion(f32[32,64,128]{2,1,0:T(8,128)S(1)} %fusion.24, bf16[32,64,128]{2,1,0:T(8,128)(2,1)S(1)} %copy-done, bf16[128,128]{1,0:T(8,128)(2,1)} %param.11), kind=kOutput, calls=%fused_computation.22 | convolution fusion | flops 68419584 | bytes 2129920 | tf_op jit(solution)/shard_map/ijc,cd->ijd/dot_general | solution.py:19
  9.8 1.6 %copy.25 = bf16[32,64,128]{1,0,2:T(8,128)(2,1)S(1)} copy(bf16[32,64,128]{2,1,0:T(8,128)(2,1)S(1)} %fusion.14) | data formatting | bytes 1048576 | tf_op jit(solution)/shard_map/convert_element_type | solution.py:25
  11.4 0.7 reshape.28
  12.2 14.7 %all_to_all.45 = bf16[8,2,16384]{2,1,0:T(2,128)(2,1)S(1)} all-to-all(bf16[8,2,16384]{2,1,0:T(2,128)(2,1)S(1)} %reshape.28), channel_id=1, replica_groups=mesh['pr'=8,'pc'=4] {'pr'}, dimensions={0} | all-to-all | bytes 1048576 | tf_op jit(solution)/shard_map/all_to_all | solution.py:45
  26.8 0.7 reshape.29
  27.5 0.0 copy-start.1
  27.5 0.4 copy.27
  27.9 0.0 copy-start.4
  28.0 1.6 %copy.28 = bf16[256,64,16]{0,1,2:T(8,128)(2,1)} copy(bf16[256,64,16]{1,2,0:T(8,128)(2,1)S(1)} %bitcast.66) | data formatting | bytes 1048576 | tf_op jit(solution)/shard_map/all_to_all | solution.py:45
  29.6 0.0 all-gather.2.cloned.1.call-update
  29.6 0.0 copy-done.1
  29.6 0.3 fusion.27
  29.9 0.0 copy-done.4
  29.9 0.4 fusion.15
  30.4 1.6 %copy.22 = bf16[32,64,128]{1,0,2:T(8,128)(2,1)S(1)} copy(bf16[32,64,128]{2,1,0:T(8,128)(2,1)S(1)} %fusion.15) | data formatting | bytes 1048576 | tf_op jit(solution)/shard_map/convert_element_type | solution.py:25
  32.0 0.7 reshape.30
  32.7 12.1 %all_to_all.46 = bf16[8,2,16384]{2,1,0:T(2,128)(2,1)S(1)} all-to-all(bf16[8,2,16384]{2,1,0:T(2,128)(2,1)S(1)} %reshape.30), channel_id=1, replica_groups=mesh['pr'=8,'pc'=4] {'pr'}, dimensions={0} | all-to-all | bytes 1048576 | tf_op jit(solution)/shard_map/all_to_all | solution.py:46
  44.8 0.7 reshape.31
  45.5 0.4 copy.24
  45.9 28.9 %all-gather.2.cloned.1.call-done = bf16[256,256,16]{0,1,2:T(8,128)(2,1)} async-done(((bf16[256,64,16]{0,1,2:T(8,128)(2,1)}), bf16[256,256,16]{0,1,2:T(8,128)(2,1)}) %all-gather.2.cloned.1.call-update) | async-done | bytes 2097168 | tf_op jit(solution)/shard_map/all_gather | solution.py:50
  74.8 2.4 %fusion.18 = bf16[256,64,16]{0,1,2:T(8,128)(2,1)S(1)} fusion(bf16[256,256,16]{0,1,2:T(8,128)(2,1)} %all-gather.2.cloned.1.call-done, bf16[256,64,16]{1,2,0:T(8,128)(2,1)S(1)} %bitcast.61), kind=kOutput, calls=%fused_computation.26 | convolution fusion | flops 134742016 | bytes 3145728 | tf_op jit(solution)/shard_map/kid,kjd->ijd/dot_general | solution.py:48
  77.2 0.0 copy-start.5
  77.2 1.0 copy.30
  78.1 1.5 %reshape.32 = bf16[8,2,16384]{2,1,0:T(2,128)(2,1)} reshape(bf16[256,16,64]{2,1,0:T(8,128)(2,1)S(1)} %bitcast.64) | data formatting | bytes 1048576
  79.6 3.7 %all-to-all-start.2 = ((bf16[8,2,16384]{2,1,0:T(2,128)(2,1)}), bf16[8,2,16384]{2,1,0:T(2,128)(2,1)S(1)}, u32[]{:S(2)}, u32[]{:S(2)}) async-start(bf16[8,2,16384]{2,1,0:T(2,128)(2,1)} %reshape.32), calls=%async_computation.2 | async-start | bytes 1048576 | tf_op jit(solution)/shard_map/all_to_all | solution.py:55
  83.3 0.0 copy-done.5
  83.3 0.4 fusion.13
  83.8 9.3 %all-to-all-done.2 = bf16[8,2,16384]{2,1,0:T(2,128)(2,1)S(1)} async-done(((bf16[8,2,16384]{2,1,0:T(2,128)(2,1)}), bf16[8,2,16384]{2,1,0:T(2,128)(2,1)S(1)}, u32[]{:S(2)}, u32[]{:S(2)}) %all-to-all-start.2) | async-done | bytes 524320 | tf_op jit(solution)/shard_map/all_to_all | solution.py:55
  93.0 0.7 reshape.33
  93.7 0.2 convert_bitcast_fusion
  93.9 0.2 fusion.19
  94.1 0.4 multiply_reduce_fusion
  94.5 0.0 copy-start.3
  94.5 0.3 copy.31
  94.8 0.4 copy-done.3
  95.2 0.0 copy-start.2
  95.2 0.5 fusion.2
  95.6 0.3 copy-done.2
  95.9 1.3 %fusion.17 = bf16[32,64,128]{2,1,0:T(8,128)(2,1)} fusion(f32[32,64,128]{2,1,0:T(8,128)S(1)} %fusion.13, bf16[32,64,128]{1,2,0:T(8,128)(2,1)S(1)} %fusion.2, bf16[128,128]{1,0:T(8,128)(2,1)S(1)} %copy-done.2), kind=kOutput, calls=%fused_computation.25 | convolution fusion | flops 67633152 | bytes 2129920 | tf_op jit(solution)/shard_map/ijd,dc->ijc/dot_general | solution.py:35
  (2 shorter events, 0.0 us)
Async XLA Ops:
  6.5 1.0 %copy-start = (bf16[32,64,128]{2,1,0:T(8,128)(2,1)S(1)}, bf16[32,64,128]{2,1,0:T(8,128)(2,1)}, u32[]{:S(2)}) copy-start(bf16[32,64,128]{2,1,0:T(8,128)(2,1)} %param.8) | copy-start | bytes 1572868
  6.5 68.3 %all-gather.2.cloned.1.call-start = ((), (), s32[]{:S(2)}) async-start(), calls=%async_computation.3 | async-start | bytes 2621440 | tf_op jit(solution)/shard_map/all_gather | solution.py:50
  27.5 2.1 %copy-start.1 = (bf16[128,128]{1,0:T(8,128)(2,1)S(1)}, bf16[128,128]{1,0:T(8,128)(2,1)}, u32[]{:S(2)}) copy-start(bf16[128,128]{1,0:T(8,128)(2,1)} %param.10) | copy-start | bytes 98308
  27.9 2.0 %copy-start.4 = (bf16[128,128]{1,0:T(8,128)(2,1)S(1)}, bf16[128,128]{1,0:T(8,128)(2,1)}, u32[]{:S(2)}) copy-start(bf16[128,128]{1,0:T(8,128)(2,1)} %param.12) | copy-start | bytes 98308
  77.2 6.2 %copy-start.5 = (bf16[128,128]{1,0:T(8,128)(2,1)S(1)}, bf16[128,128]{1,0:T(8,128)(2,1)}, u32[]{:S(2)}) copy-start(bf16[128,128]{1,0:T(8,128)(2,1)} %param.15) | copy-start | bytes 98308
  79.6 13.4 %all-to-all-start.2 = ((bf16[8,2,16384]{2,1,0:T(2,128)(2,1)}), bf16[8,2,16384]{2,1,0:T(2,128)(2,1)S(1)}, u32[]{:S(2)}, u32[]{:S(2)}) async-start(bf16[8,2,16384]{2,1,0:T(2,128)(2,1)} %reshape.32), calls=%async_computation.2 | async-start | bytes 1048576 | tf_op jit(solution)/shard_map/all_to_all | solution.py:55
  94.5 0.7 copy-start.3
  95.2 0.8 copy-start.2
Sparse Core Ops, SparseCore 0:
  29.7 45.0 all-gather.1
where the time goes:
time: 105 us; the launch traced here: 104 us
  waiting for transfers between devices  38.2 us (36%)
  blocking collectives  26.8 us (26%)
  between operations  13.6 us (13%)
  local copies, waits for them, and re-layouts  13.5 us (13%)
  matrix products  6.96 us (7%)
  starting transfers between devices  3.68 us (4%)
  other arithmetic  1.27 us (1%)
    all_gather x1, waiting for transfers between devices, on_device(): lax.all_gather(left_lines, 'pc', axis=1, tiled=True)  28.9 us
    all_to_all x1, blocking collectives, on_device(): lax.all_to_all(left, 'pr', split_axis=2, concat_axis=0, tiled=True)  14.7 us
    all_to_all x1, blocking collectives, on_device(): lax.all_to_all(right, 'pr', split_axis=2, concat_axis=0, tiled=True)  12.1 us
    all_to_all x1, waiting for transfers between devices, on_device(): mixed = lax.all_to_all(strip, 'pr', split_axis=0, concat_axis=2, tiled=True)  9.25 us
    unnamed x18, local copies, waits for them, and re-layouts  6.59 us
    all_to_all x1, starting transfers between devices, on_device(): mixed = lax.all_to_all(strip, 'pr', split_axis=0, concat_axis=2, tiled=True)  3.67 us
    convert_element_type x2, local copies, waits for them, and re-layouts, make_factors(): return (pair_in, left.astype(jnp.bfloat16), right.astype(jnp.bfloat16))  3.24 us
    dot_general x1, matrix products, on_device(): jnp.einsum('kid,kjd->ijd', lax.all_gather(left_lines, 'pc', axis=1, tiled...  2.35 us
  transfers between devices with their start and end apart: 2, of which 2 were waited for; matrix products, arithmetic and copies ran while one was open for 4% of the time, Pallas kernels for 0%

commit v1 on v0

--- a/solution.py
+++ b/solution.py
@@ -47,7 +47,9 @@
     )
     strip = jnp.einsum(
         "kid,kjd->ijd",
-        lax.all_gather(left_lines, "pc", axis=1, tiled=True),
+        jnp.concatenate(
+            lax.all_to_all(jnp.stack([left_lines] * lax.axis_size("pc")), "pc", 0, 0), axis=1
+        ),
         right_lines,
         preferred_element_type=jnp.float32,
     )

time: 105 us -> 111 us (1.057)
  waiting for transfers between devices: 38.2 us -> 67.3 us
  blocking collectives: 26.8 us -> 0 us
  starting transfers between devices: 3.68 us -> 17.9 us
  between operations: 13.6 us -> 0.21 us
  local copies, waits for them, and re-layouts: 13.5 us -> 16.3 us
    all_to_all x0 -> x3, waiting for transfers between devices: none -> 58 us  [the longest x1 45 us: on_device(): lax.all_to_all(jnp.stack([left_lines] * lax.axis_size('pc')), 'pc', 0, 0)]
    all_gather x1 -> x0, waiting for transfers between devices: 28.9 us -> none  [on_device(): lax.all_gather(left_lines, 'pc', axis=1, tiled=True)]
    all_to_all x2 -> x0, blocking collectives: 26.8 us -> none  [the longest x1 14.7 us: on_device(): lax.all_to_all(left, 'pr', split_axis=2, concat_axis=0, tiled=True)]
    all_to_all x0 -> x3, starting transfers between devices: none -> 13.6 us  [the longest x1 5.18 us: on_device(): lax.all_to_all(left, 'pr', split_axis=2, concat_axis=0, tiled=True)]
    another operation x0 -> x2, local copies, waits for them, and re-layouts: none -> 2.81 us  [on_device(): jnp.stack([left_lines] * lax.axis_size('pc'))]
    all_to_all x2 -> x1, local copies, waits for them, and re-layouts: 2.06 us -> 0.41 us  [on_device(): lax.all_to_all(left, 'pr', split_axis=2, concat_axis=0, tiled=True)]
    unnamed x18, local copies, waits for them, and re-layouts: 6.59 us -> 8.2 us
  transfers between devices with their start and end apart: 2 -> 4, of which waited for: 2 -> 4; matrix products, arithmetic and copies ran while one was open for 4% -> 7% of each run, Pallas kernels for 0% -> 0%
where the time goes in v1:
time: 111 us; the launch traced here: 110 us
  waiting for transfers between devices  67.3 us (61%)
  starting transfers between devices  17.9 us (16%)
  local copies, waits for them, and re-layouts  16.3 us (15%)
  matrix products  7.16 us (6%)
  other arithmetic  1.27 us (1%)
    all_to_all x1, waiting for transfers between devices, on_device(): lax.all_to_all(jnp.stack([left_lines] * lax.axis_size('pc')), 'pc', 0, 0)  45 us
    all_to_all x1, waiting for transfers between devices, on_device(): mixed = lax.all_to_all(strip, 'pr', split_axis=0, concat_axis=2, tiled=True)  9.28 us
    unnamed x18, local copies, waits for them, and re-layouts  8.2 us
    all_to_all x1, waiting for transfers between devices, on_device(): lax.all_to_all(right, 'pr', split_axis=2, concat_axis=0, tiled=True)  7.22 us
    all_to_all x1, waiting for transfers between devices, on_device(): lax.all_to_all(left, 'pr', split_axis=2, concat_axis=0, tiled=True)  5.83 us
    all_to_all x1, starting transfers between devices, on_device(): lax.all_to_all(left, 'pr', split_axis=2, concat_axis=0, tiled=True)  5.18 us
    all_to_all x1, starting transfers between devices, on_device(): lax.all_to_all(jnp.stack([left_lines] * lax.axis_size('pc')), 'pc', 0, 0)  4.87 us
    all_to_all x1, starting transfers between devices, on_device(): mixed = lax.all_to_all(strip, 'pr', split_axis=0, concat_axis=2, tiled=True)  4.31 us
  transfers between devices with their start and end apart: 4, of which 4 were waited for; matrix products, arithmetic and copies ran while one was open for 7% of the time, Pallas kernels for 0%

profile of v1, /device:TPU:0, one launch (start us, length us, event | category | flops | bytes accessed | tf_op | source)
XLA Modules:
  0.0 110.1 jit_solution(14420731460168739265)
XLA Ops:
  0.0 0.0 copy-start
  0.0 1.0 copy-done
  1.0 1.0 fusion.33
  2.1 1.2 %fusion.19 = bf16[32,64,128]{2,1,0:T(8,128)(2,1)S(1)} fusion(f32[32,64,128]{2,1,0:T(8,128)S(1)} %fusion.33, bf16[32,64,128]{2,1,0:T(8,128)(2,1)S(1)} %copy-done, bf16[128,128]{1,0:T(8,128)(2,1)} %param.11), kind=kOutput, calls=%fused_computation.24 | convolution fusion | flops 68419584 | bytes 2129920 | tf_op jit(solution)/shard_map/ijc,cd->ijd/dot_general | solution.py:19
  3.3 0.0 copy-start.1
  3.3 1.6 %copy.25 = bf16[32,64,128]{1,0,2:T(8,128)(2,1)S(1)} copy(bf16[32,64,128]{2,1,0:T(8,128)(2,1)S(1)} %fusion.19) | data formatting | bytes 1048576 | tf_op jit(solution)/shard_map/convert_element_type | solution.py:25
  4.9 0.0 copy-start.4
  4.9 1.5 %reshape.39 = bf16[8,2,16384]{2,1,0:T(2,128)(2,1)} reshape(bf16[128,32,64]{2,1,0:T(8,128)(2,1)S(1)} %bitcast.63) | data formatting | bytes 1048576
  6.4 5.2 %all-to-all-start.1 = ((bf16[8,2,16384]{2,1,0:T(2,128)(2,1)}), bf16[8,2,16384]{2,1,0:T(2,128)(2,1)S(1)}, u32[]{:S(2)}, u32[]{:S(2)}) async-start(bf16[8,2,16384]{2,1,0:T(2,128)(2,1)} %reshape.39), calls=%async_computation.1 | async-start | bytes 1048576 | tf_op jit(solution)/shard_map/all_to_all | solution.py:45
  11.6 0.0 copy-done.1
  11.6 0.3 fusion.36
  11.9 0.0 copy-done.4
  11.9 0.4 fusion.20
  12.4 1.6 %copy.22 = bf16[32,64,128]{1,0,2:T(8,128)(2,1)S(1)} copy(bf16[32,64,128]{2,1,0:T(8,128)(2,1)S(1)} %fusion.20) | data formatting | bytes 1048576 | tf_op jit(solution)/shard_map/convert_element_type | solution.py:25
  14.0 1.5 %reshape.41 = bf16[8,2,16384]{2,1,0:T(2,128)(2,1)} reshape(bf16[128,32,64]{2,1,0:T(8,128)(2,1)S(1)} %bitcast.64) | data formatting | bytes 1048576
  15.5 5.8 %all-to-all-done.1 = bf16[8,2,16384]{2,1,0:T(2,128)(2,1)S(1)} async-done(((bf16[8,2,16384]{2,1,0:T(2,128)(2,1)}), bf16[8,2,16384]{2,1,0:T(2,128)(2,1)S(1)}, u32[]{:S(2)}, u32[]{:S(2)}) %all-to-all-start.1) | async-done | bytes 524320 | tf_op jit(solution)/shard_map/all_to_all | solution.py:45
  21.3 3.5 %all-to-all-start = ((bf16[8,2,16384]{2,1,0:T(2,128)(2,1)}), bf16[8,2,16384]{2,1,0:T(2,128)(2,1)S(1)}, u32[]{:S(2)}, u32[]{:S(2)}) async-start(bf16[8,2,16384]{2,1,0:T(2,128)(2,1)} %reshape.41), calls=%async_computation | async-start | bytes 1048576 | tf_op jit(solution)/shard_map/all_to_all | solution.py:46
  24.8 0.7 reshape.40
  25.5 0.4 copy.27
  25.9 1.3 %copy.28 = bf16[256,64,16]{0,2,1:T(8,128)(2,1)S(1)} copy(bf16[256,64,16]{1,2,0:T(8,128)(2,1)S(1)} %bitcast.67) | data formatting | bytes 1048576 | tf_op jit(solution)/shard_map/stack | solution.py:51
  27.3 7.2 %all-to-all-done = bf16[8,2,16384]{2,1,0:T(2,128)(2,1)S(1)} async-done(((bf16[8,2,16384]{2,1,0:T(2,128)(2,1)}), bf16[8,2,16384]{2,1,0:T(2,128)(2,1)S(1)}, u32[]{:S(2)}, u32[]{:S(2)}) %all-to-all-start) | async-done | bytes 524320 | tf_op jit(solution)/shard_map/all_to_all | solution.py:46
  34.5 1.5 %stack.10 = bf16[4,256,64,16]{1,3,2,0:T(8,128)(2,1)} broadcast(bf16[256,64,16]{0,2,1:T(8,128)(2,1)S(1)} %copy.28), dimensions={1,2,3} | broadcast | bytes 2621440 | tf_op jit(solution)/shard_map/stack | solution.py:51
  36.0 4.9 %all-to-all-start.2 = ((bf16[4,256,64,16]{1,3,2,0:T(8,128)(2,1)}), bf16[4,256,64,16]{1,3,2,0:T(8,128)(2,1)}, u32[]{:S(2)}, u32[]{:S(2)}) async-start(bf16[4,256,64,16]{1,3,2,0:T(8,128)(2,1)} %stack.10), calls=%async_computation.2 | async-start | bytes 4194304 | tf_op jit(solution)/shard_map/all_to_all | solution.py:51
  40.8 0.7 reshape.42
  41.5 0.4 copy.24
  41.9 45.0 %all-to-all-done.2 = bf16[4,256,64,16]{1,3,2,0:T(8,128)(2,1)} async-done(((bf16[4,256,64,16]{1,3,2,0:T(8,128)(2,1)}), bf16[4,256,64,16]{1,3,2,0:T(8,128)(2,1)}, u32[]{:S(2)}, u32[]{:S(2)}) %all-to-all-start.2) | async-done | bytes 2097184 | tf_op jit(solution)/shard_map/all_to_all | solution.py:51
  86.9 2.5 %fusion.25 = bf16[256,64,16]{0,1,2:T(8,128)(2,1)S(1)} fusion(bf16[256,256,16]{0,2,1:T(8,128)(2,1)} %bitcast.13, bf16[256,64,16]{1,2,0:T(8,128)(2,1)S(1)} %bitcast.69), kind=kOutput, calls=%fused_computation.28 | convolution fusion | flops 134742016 | bytes 3145728 | tf_op jit(solution)/shard_map/kid,kjd->ijd/dot_general | solution.py:48
  89.4 0.0 copy-start.5
  89.4 1.0 copy.31
  90.4 1.5 %reshape.43 = bf16[8,2,16384]{2,1,0:T(2,128)(2,1)} reshape(bf16[256,16,64]{2,1,0:T(8,128)(2,1)S(1)} %bitcast.65) | data formatting | bytes 1048576
  91.9 4.3 %all-to-all-start.3 = ((bf16[8,2,16384]{2,1,0:T(2,128)(2,1)}), bf16[8,2,16384]{2,1,0:T(2,128)(2,1)S(1)}, u32[]{:S(2)}, u32[]{:S(2)}) async-start(bf16[8,2,16384]{2,1,0:T(2,128)(2,1)} %reshape.43), calls=%async_computation.3 | async-start | bytes 1048576 | tf_op jit(solution)/shard_map/all_to_all | solution.py:57
  96.2 0.0 copy-done.5
  96.2 0.4 fusion.18
  96.6 9.3 %all-to-all-done.3 = bf16[8,2,16384]{2,1,0:T(2,128)(2,1)S(1)} async-done(((bf16[8,2,16384]{2,1,0:T(2,128)(2,1)}), bf16[8,2,16384]{2,1,0:T(2,128)(2,1)S(1)}, u32[]{:S(2)}, u32[]{:S(2)}) %all-to-all-start.3) | async-done | bytes 524320 | tf_op jit(solution)/shard_map/all_to_all | solution.py:57
  105.9 0.7 reshape.44
  106.6 0.2 convert_bitcast_fusion
  106.8 0.2 fusion.28
  107.0 0.4 multiply_reduce_fusion
  107.4 0.0 copy-start.3
  107.4 0.3 copy.32
  107.7 0.4 copy-done.3
  108.1 0.0 copy-start.2
  108.1 0.5 fusion.2
  108.5 0.3 copy-done.2
  108.8 1.3 %fusion.21 = bf16[32,64,128]{2,1,0:T(8,128)(2,1)} fusion(f32[32,64,128]{2,1,0:T(8,128)S(1)} %fusion.18, bf16[32,64,128]{1,2,0:T(8,128)(2,1)S(1)} %fusion.2, bf16[128,128]{1,0:T(8,128)(2,1)S(1)} %copy-done.2), kind=kOutput, calls=%fused_computation.26 | convolution fusion | flops 67633152 | bytes 2129920 | tf_op jit(solution)/shard_map/ijd,dc->ijc/dot_general | solution.py:35
  (2 shorter events, 0.0 us)
Async XLA Ops:
  0.0 1.0 copy-start
  3.3 8.3 %copy-start.1 = (bf16[128,128]{1,0:T(8,128)(2,1)S(1)}, bf16[128,128]{1,0:T(8,128)(2,1)}, u32[]{:S(2)}) copy-start(bf16[128,128]{1,0:T(8,128)(2,1)} %param.10) | copy-start | bytes 98308
  4.9 7.0 %copy-start.4 = (bf16[128,128]{1,0:T(8,128)(2,1)S(1)}, bf16[128,128]{1,0:T(8,128)(2,1)}, u32[]{:S(2)}) copy-start(bf16[128,128]{1,0:T(8,128)(2,1)} %param.12) | copy-start | bytes 98308
  6.4 14.9 %all-to-all-start.1 = ((bf16[8,2,16384]{2,1,0:T(2,128)(2,1)}), bf16[8,2,16384]{2,1,0:T(2,128)(2,1)S(1)}, u32[]{:S(2)}, u32[]{:S(2)}) async-start(bf16[8,2,16384]{2,1,0:T(2,128)(2,1)} %reshape.39), calls=%async_computation.1 | async-start | bytes 1048576 | tf_op jit(solution)/shard_map/all_to_all | solution.py:45
  21.3 13.1 %all-to-all-start = ((bf16[8,2,16384]{2,1,0:T(2,128)(2,1)}), bf16[8,2,16384]{2,1,0:T(2,128)(2,1)S(1)}, u32[]{:S(2)}, u32[]{:S(2)}) async-start(bf16[8,2,16384]{2,1,0:T(2,128)(2,1)} %reshape.41), calls=%async_computation | async-start | bytes 1048576 | tf_op jit(solution)/shard_map/all_to_all | solution.py:46
  36.0 50.9 %all-to-all-start.2 = ((bf16[4,256,64,16]{1,3,2,0:T(8,128)(2,1)}), bf16[4,256,64,16]{1,3,2,0:T(8,128)(2,1)}, u32[]{:S(2)}, u32[]{:S(2)}) async-start(bf16[4,256,64,16]{1,3,2,0:T(8,128)(2,1)} %stack.10), calls=%async_computation.2 | async-start | bytes 4194304 | tf_op jit(solution)/shard_map/all_to_all | solution.py:51
  89.4 6.8 %copy-start.5 = (bf16[128,128]{1,0:T(8,128)(2,1)S(1)}, bf16[128,128]{1,0:T(8,128)(2,1)}, u32[]{:S(2)}) copy-start(bf16[128,128]{1,0:T(8,128)(2,1)} %param.15) | copy-start | bytes 98308
  91.9 14.0 %all-to-all-start.3 = ((bf16[8,2,16384]{2,1,0:T(2,128)(2,1)}), bf16[8,2,16384]{2,1,0:T(2,128)(2,1)S(1)}, u32[]{:S(2)}, u32[]{:S(2)}) async-start(bf16[8,2,16384]{2,1,0:T(2,128)(2,1)} %reshape.43), calls=%async_computation.3 | async-start | bytes 1048576 | tf_op jit(solution)/shard_map/all_to_all | solution.py:57
  107.4 0.7 copy-start.3
  108.1 0.8 copy-start.2
